TPU v7x, 32 devices: a whole 2x2x4 slice. The times are simulated.
32 devices in a mesh: row: 8 (over z, x), mem: 2 (over core), lev: 2 (over y).
Axes of the slice: x: 2, y: 2, z: 4, core: 2. Of those that a mesh axis runs over, the one named last changes fastest.
Arguments:
- control_fields: bfloat16 [4, 6, 256, 2048], P('mem', 'lev', 'row'), may hold values from -6 to 6
- perturbations: bfloat16 [3, 4, 6, 256, 2048], P(None, 'mem', 'lev', 'row'), may hold values from -3 to 3
- column_taper: bfloat16 [2048, 2048], P('row'), may hold values from -1 to 2, as said below
- row_taper: bfloat16 [256, 256], P('row'), may hold values from -1 to 2, as said below
- courant_numbers: float32 [3, 6, 256, 2048], P(None, 'lev', 'row', 'mem'), may hold values from -0.3 to 0.3
- tracer_slope: float32 [2, 6, 256, 2048], P(None, 'lev', 'row', 'mem'), may hold values from -3 to 3
Outputs:
- increment: float32 [3, 6, 256, 2048], P(None, 'lev', 'row', 'mem')
Inputs may be any that keep to these rules, and one draw needn't show every extreme that they name: `column_taper`: A square matrix. `row_taper`: A square matrix.
All inputs are finite; a program needn't handle non-finite values.
Results may differ from a plain program's by a relative error of at most 0.0048.
Values may be sent and summed in bfloat16 or wider, within the bound.
A program may use at most 64 MiB of HBM per device.

v0:
```python
import jax
import jax.numpy as jnp
from jax import lax
from jax.sharding import PartitionSpec as P

STEPS = 4


def extended(block, sides, width):
    for axis, dim in sides:
        count = lax.axis_size(axis)
        forward = [(i, i + 1) for i in range(count - 1)]
        backward = [(target, source) for source, target in forward]
        low = lax.ppermute(
            lax.slice_in_dim(block, block.shape[dim] - width, None, axis=dim), axis, forward
        )
        high = lax.ppermute(lax.slice_in_dim(block, 0, width, axis=dim), axis, backward)
        block = jnp.concatenate([low, block, high], axis=dim)
    return block


def upwind(middle, behind, forward, velocity):
    return jnp.maximum(velocity, 0.0) * (middle - behind) + jnp.minimum(velocity, 0.0) * (
        forward - middle
    )


def advance(present, courant_numbers, tracer_slope, padded):
    middle = padded[:, 1:-1, 1:-1, 1:-1]
    change = upwind(
        middle, padded[:, :-2, 1:-1, 1:-1], padded[:, 2:, 1:-1, 1:-1], courant_numbers[0]
    )
    change = change + upwind(
        middle, padded[:, 1:-1, :-2, 1:-1], padded[:, 1:-1, 2:, 1:-1], courant_numbers[1]
    )
    change = change + upwind(
        middle, padded[:, 1:-1, 1:-1, :-2], padded[:, 1:-1, 1:-1, 2:], courant_numbers[2]
    )
    shifted = present - change
    source = present[0] * tracer_slope[0] + present[1] * tracer_slope[1]
    return jnp.concatenate([shifted[:2], shifted[2:] - source[None]], axis=0)


def on_device(
    control_fields, perturbations, column_taper, row_taper, courant_numbers, tracer_slope
):
    member_count, level_count, row_count, column_count = control_fields.shape
    field_count = member_count * level_count
    flattened = control_fields.reshape(field_count * row_count, column_count)
    block_width = column_count // lax.axis_size("mem")
    own_block = lax.dynamic_slice_in_dim(
        column_taper, lax.axis_index("mem") * block_width, block_width, 1
    )
    column_block = lax.all_gather(own_block, "row", axis=0, tiled=True)
    first_pass = jnp.dot(
        flattened,
        lax.all_gather(column_block, "mem", axis=1, tiled=True),
        preferred_element_type=jnp.float32,
    )
    first_pass = first_pass.astype(jnp.bfloat16).reshape(field_count, row_count, column_count)
    row_whole = lax.all_gather(row_taper, "row", axis=0, tiled=True)
    tapered = jnp.einsum(
        "ij,fjc->fic",
        row_whole,
        lax.all_to_all(first_pass, "row", split_axis=2, concat_axis=1, tiled=True),
        preferred_element_type=jnp.float32,
    )
    localized = lax.all_to_all(
        tapered.astype(jnp.bfloat16), "row", split_axis=1, concat_axis=2, tiled=True
    )
    localized = localized.reshape(member_count, level_count, row_count, column_count)
    weighted = jnp.einsum(
        "kmlrc,mlrc->klrc", perturbations, localized, preferred_element_type=jnp.float32
    )
    summed = lax.psum(weighted, "mem")
    own_columns = column_count // lax.axis_size("mem")
    margin = STEPS
    widened = jnp.pad(summed, ((0, 0), (0, 0), (0, 0), (margin, margin)))
    present = lax.dynamic_slice_in_dim(
        widened, lax.axis_index("mem") * own_columns, own_columns + 2 * margin, 3
    )
    background = jnp.concatenate([courant_numbers, tracer_slope], axis=0)
    background = extended(background, (("mem", 3),), margin - 1)
    background = jnp.pad(background, ((0, 0), (0, 0), (0, 0), (1, 1)))
    courant_near = background[:3]
    slope_near = background[3:]
    for advect_step in range(STEPS):
        padded = extended(present, (("row", 2), ("lev", 1)), 1)
        padded = jnp.pad(padded, ((0, 0), (0, 0), (0, 0), (1, 1)))
        present = advance(present, courant_near, slope_near, padded)
    return present[:, :, :, margin : margin + own_columns]


def solution(mesh):
    placed = (
        P("mem", "lev", "row", None),
        P(None, "mem", "lev", "row", None),
        P("row", None),
        P("row", None),
        P(None, "lev", "row", "mem"),
        P(None, "lev", "row", "mem"),
    )
    return jax.shard_map(
        on_device,
        mesh=mesh,
        in_specs=placed,
        out_specs=P(None, "lev", "row", "mem"),
        check_vma=False,
    )
```

profile of v0, /device:TPU:0, one launch (start us, length us, event | category | flops | bytes accessed | tf_op | source)
XLA Modules:
  0.0 356.1 jit_solution(13105754108425344147)
XLA Ops:
  8.7 76.3 %all-gather.3.cloned.1.call-done = bf16[2048,1024]{1,0:T(8,128)(2,1)} async-done(((bf16[256,1024]{1,0:T(8,128)(2,1)}), bf16[2048,1024]{1,0:T(8,128)(2,1)}) %all-gather.3.cloned.1.call-update) | async-done | bytes 4194320 | tf_op jit(solution)/shard_map/all_gather | solution.py:54
  85.0 19.9 %all-gather.5.cloned.1.call-done = bf16[2048,2048]{1,0:T(8,128)(2,1)} async-done(((bf16[2048,1024]{1,0:T(8,128)(2,1)}), bf16[2048,2048]{1,0:T(8,128)(2,1)}) %all-gather.5.cloned.1.call-update) | async-done | bytes 8388624 | tf_op jit(solution)/shard_map/all_gather | solution.py:57
  105.0 5.2 %convolution_convert_fusion = bf16[2048,192]{0,1:T(8,128)(2,1)S(1)} fusion(bf16[192,2048]{1,0:T(8,128)(2,1)S(1)} %bitcast.47, bf16[2048,2048]{1,0:T(8,128)(2,1)} %all-gather.5.cloned.1.call-done), kind=kOutput, calls=%fused_computation.23 | convolution fusion | flops 1611005952 | bytes 9961472 | tf_op jit(solution)/shard_map/dot_general | solution.py:55
  110.2 4.2 %copy.15 = bf16[6,32,2048]{1,0,2:T(8,128)(2,1)} copy(bf16[6,32,2048]{2,1,0:T(8,128)(2,1)S(1)} %bitcast.46) | data formatting | bytes 1572864 | tf_op jit(solution)/shard_map/reshape | solution.py:60
  114.3 5.7 %reshape.16 = bf16[8,2,24576]{2,1,0:T(2,128)(2,1)} reshape(bf16[2048,6,32]{2,1,0:T(8,128)(2,1)} %bitcast.41) | data formatting | bytes 1572864
  120.0 5.9 %all-to-all-start = ((bf16[8,2,24576]{2,1,0:T(2,128)(2,1)}), bf16[8,2,24576]{2,1,0:T(2,128)(2,1)S(1)}, u32[]{:S(2)}, u32[]{:S(2)}) async-start(bf16[8,2,24576]{2,1,0:T(2,128)(2,1)} %reshape.16), calls=%async_computation | async-start | bytes 1572864 | tf_op jit(solution)/shard_map/all_to_all | solution.py:65
  126.0 41.8 %all_gather.11 = bf16[256,256]{1,0:T(8,128)(2,1)S(1)} all-gather(bf16[32,256]{1,0:T(8,128)(2,1)S(1)} %copy-done.9), channel_id=1, replica_groups=mesh['row'=8,'mem'=2,'lev'=2] {'row'}, dimensions={0}, use_global_device_ids=true | all-gather | bytes 147456 | tf_op jit(solution)/shard_map/all_gather | solution.py:61
  167.8 4.1 %reshape.17 = bf16[2048,6,32]{2,1,0:T(8,128)(2,1)} reshape(bf16[8,2,24576]{2,1,0:T(2,128)(2,1)S(1)} %all-to-all-done) | data formatting | bytes 1572864
  171.9 4.1 %copy.17 = bf16[6,8,32,256]{3,2,1,0:T(8,128)(2,1)S(1)} copy(bf16[6,8,32,256]{2,0,3,1:T(8,128)(2,1)} %bitcast.42) | data formatting | bytes 1572864 | tf_op jit(solution)/shard_map/all_to_all | solution.py:65
  177.4 22.4 %all_to_all.33 = bf16[6,256,256]{2,0,1:T(8,128)(2,1)S(1)} all-to-all(bf16[6,256,256]{2,0,1:T(8,128)(2,1)S(1)} %copy.19), channel_id=1, replica_groups=mesh['row'=8,'mem'=2,'lev'=2] {'row'}, dimensions={1} | all-to-all | bytes 1572864 | tf_op jit(solution)/shard_map/all_to_all | solution.py:68
  205.9 19.7 %all-reduce.8.cloned.1.call-done = f32[3,3,32,2048]{3,2,1,0:T(8,128)} async-done(((f32[3,3,32,2048]{3,2,1,0:T(8,128)}), f32[3,3,32,2048]{3,2,1,0:T(8,128)}) %all-reduce.8.cloned.1.call-update) | async-done | bytes 2359312 | tf_op jit(solution)/shard_map/psum | solution.py:75
  232.5 4.2 %collective-permute-done.3 = f32[3,3,1,1032]{3,2,1,0:T(1,128)S(1)} collective-permute-done((f32[3,3,1,1032]{3,2,1,0:T(1,128)S(1)}, f32[3,3,1,1032]{3,2,1,0:T(1,128)S(1)}, u32[]{:S(2)}, u32[]{:S(2)}) %collective-permute-start.3) | collective-permute-done | bytes 37184 | tf_op jit(solution)/shard_map/ppermute | solution.py:17
  237.8 4.2 %collective-permute-start.4 = (f32[3,1,34,1032]{3,2,1,0:T(8,128)}, f32[3,1,34,1032]{3,2,1,0:T(8,128)}, u32[]{:S(2)}, u32[]{:S(2)}) collective-permute-start(f32[3,1,34,1032]{3,2,1,0:T(8,128)} %get-tuple-element.21), channel_id=1, source_target_pairs={{0,1},{2,3},{4,5},{6,7},{8,9},{10,11},{12,13},{14,15},{16,17},{18,... | collective-permute-start | bytes 1263176 | tf_op jit(solution)/shard_map/ppermute | solution.py:14
  252.3 4.9 %collective-permute-done.5 = f32[3,1,34,1032]{3,2,1,0:T(8,128)} collective-permute-done((f32[3,1,34,1032]{3,2,1,0:T(8,128)}, f32[3,1,34,1032]{3,2,1,0:T(8,128)}, u32[]{:S(2)}, u32[]{:S(2)}) %collective-permute-start.5) | collective-permute-done | bytes 421088 | tf_op jit(solution)/shard_map/ppermute | solution.py:17
  263.9 4.3 %collective-permute-start.6 = (f32[3,3,1,1032]{3,2,1,0:T(1,128)S(1)}, f32[3,3,1,1032]{3,2,1,0:T(1,128)S(1)}, u32[]{:S(2)}, u32[]{:S(2)}) collective-permute-start(f32[3,3,1,1032]{3,2,1,0:T(1,128)S(1)} %get-tuple-element.27), channel_id=1, source_target_pairs={{0,4},{4,8},{8,12},{12,16},{16,20},{20,24},{24,28},{1,5},{5,9},{9,... | collective-permute-start | bytes 111464 | tf_op jit(solution)/shard_map/ppermute | solution.py:14
  277.1 8.5 %collective-permute-done.8 = f32[3,1,34,1032]{3,2,1,0:T(8,128)S(1)} collective-permute-done((f32[3,1,34,1032]{3,2,1,0:T(8,128)S(1)}, f32[3,1,34,1032]{3,2,1,0:T(8,128)S(1)}, u32[]{:S(2)}, u32[]{:S(2)}) %collective-permute-start.8) | collective-permute-done | bytes 421088 | tf_op jit(solution)/shard_map/ppermute | solution.py:14
  285.6 4.1 %collective-permute-done.9 = f32[3,1,34,1032]{3,2,1,0:T(8,128)S(1)} collective-permute-done((f32[3,1,34,1032]{3,2,1,0:T(8,128)S(1)}, f32[3,1,34,1032]{3,2,1,0:T(8,128)S(1)}, u32[]{:S(2)}, u32[]{:S(2)}) %collective-permute-start.9) | collective-permute-done | bytes 421088 | tf_op jit(solution)/shard_map/ppermute | solution.py:17
  299.2 4.1 %collective-permute-done.11 = f32[3,3,1,1032]{3,2,1,0:T(1,128)S(1)} collective-permute-done((f32[3,3,1,1032]{3,2,1,0:T(1,128)S(1)}, f32[3,3,1,1032]{3,2,1,0:T(1,128)S(1)}, u32[]{:S(2)}, u32[]{:S(2)}) %collective-permute-start.11) | collective-permute-done | bytes 37184 | tf_op jit(solution)/shard_map/ppermute | solution.py:17
  306.2 6.1 %collective-permute-done.12 = f32[3,1,34,1032]{3,2,1,0:T(8,128)S(1)} collective-permute-done((f32[3,1,34,1032]{3,2,1,0:T(8,128)S(1)}, f32[3,1,34,1032]{3,2,1,0:T(8,128)S(1)}, u32[]{:S(2)}, u32[]{:S(2)}) %collective-permute-start.12) | collective-permute-done | bytes 421088 | tf_op jit(solution)/shard_map/ppermute | solution.py:14
  312.3 4.1 %collective-permute-done.13 = f32[3,1,34,1032]{3,2,1,0:T(8,128)S(1)} collective-permute-done((f32[3,1,34,1032]{3,2,1,0:T(8,128)S(1)}, f32[3,1,34,1032]{3,2,1,0:T(8,128)S(1)}, u32[]{:S(2)}, u32[]{:S(2)}) %collective-permute-start.13) | collective-permute-done | bytes 421088 | tf_op jit(solution)/shard_map/ppermute | solution.py:17
  320.7 4.3 %collective-permute-start.14 = (f32[3,3,1,1032]{3,2,1,0:T(1,128)S(1)}, f32[3,3,1,1032]{3,2,1,0:T(1,128)S(1)}, u32[]{:S(2)}, u32[]{:S(2)}) collective-permute-start(f32[3,3,1,1032]{3,2,1,0:T(1,128)S(1)} %get-tuple-element.23), channel_id=1, source_target_pairs={{0,4},{4,8},{8,12},{12,16},{16,20},{20,24},{24,28},{1,5},{5,9},{9,... | collective-permute-start | bytes 111464 | tf_op jit(solution)/shard_map/ppermute | solution.py:14
  326.7 4.2 %collective-permute-done.15 = f32[3,3,1,1032]{3,2,1,0:T(1,128)S(1)} collective-permute-done((f32[3,3,1,1032]{3,2,1,0:T(1,128)S(1)}, f32[3,3,1,1032]{3,2,1,0:T(1,128)S(1)}, u32[]{:S(2)}, u32[]{:S(2)}) %collective-permute-start.15) | collective-permute-done | bytes 37184 | tf_op jit(solution)/shard_map/ppermute | solution.py:17
  334.1 5.4 %collective-permute-done.16 = f32[3,1,34,1032]{3,2,1,0:T(8,128)S(1)} collective-permute-done((f32[3,1,34,1032]{3,2,1,0:T(8,128)S(1)}, f32[3,1,34,1032]{3,2,1,0:T(8,128)S(1)}, u32[]{:S(2)}, u32[]{:S(2)}) %collective-permute-start.16) | collective-permute-done | bytes 421088 | tf_op jit(solution)/shard_map/ppermute | solution.py:14
  339.5 4.4 %collective-permute-done.17 = f32[3,1,34,1032]{3,2,1,0:T(8,128)S(1)} collective-permute-done((f32[3,1,34,1032]{3,2,1,0:T(8,128)S(1)}, f32[3,1,34,1032]{3,2,1,0:T(8,128)S(1)}, u32[]{:S(2)}, u32[]{:S(2)}) %collective-permute-start.17) | collective-permute-done | bytes 421088 | tf_op jit(solution)/shard_map/ppermute | solution.py:17
  (90 shorter events, 70.3 us)
Async XLA Ops:
  6.5 78.5 %all-gather.3.cloned.1.call-start = ((), (), s32[]{:S(2)}) async-start(), calls=%async_computation.2 | async-start | bytes 4718592 | tf_op jit(solution)/shard_map/all_gather | solution.py:54
  8.6 96.3 %all-gather.5.cloned.1.call-start = ((), (), s32[]{:S(2)}) async-start(), calls=%async_computation.3 | async-start | bytes 12582912 | tf_op jit(solution)/shard_map/all_gather | solution.py:57
  85.0 20.0 %copy-start.10 = (bf16[2,3,32,2048]{3,2,1,0:T(8,128)(2,1)S(1)}, bf16[2,3,32,2048]{3,2,1,0:T(8,128)(2,1)}, u32[]{:S(2)}) copy-start(bf16[2,3,32,2048]{3,2,1,0:T(8,128)(2,1)} %param.6) | copy-start | bytes 2359300
  120.0 47.8 %all-to-all-start = ((bf16[8,2,24576]{2,1,0:T(2,128)(2,1)}), bf16[8,2,24576]{2,1,0:T(2,128)(2,1)S(1)}, u32[]{:S(2)}, u32[]{:S(2)}) async-start(bf16[8,2,24576]{2,1,0:T(2,128)(2,1)} %reshape.16), calls=%async_computation | async-start | bytes 1572864 | tf_op jit(solution)/shard_map/all_to_all | solution.py:65
  125.9 99.7 %all-reduce.8.cloned.1.call-start = ((), (), s32[]{:S(2)}) async-start(), calls=%async_computation.4 | async-start | bytes 4718592 | tf_op jit(solution)/shard_map/psum | solution.py:75
  205.9 37.4 %copy-start.6 = (f32[5,3,32,1024]{3,2,1,0:T(8,128)}, f32[5,3,32,1024]{3,2,1,0:T(8,128)S(1)}, u32[]{:S(2)}) copy-start(f32[5,3,32,1024]{3,2,1,0:T(8,128)S(1)} %constant_dynamic-update-slice_fusion) | copy-start | bytes 5898244
  227.1 5.4 %collective-permute-start.2 = (f32[3,3,1,1032]{3,2,1,0:T(1,128)S(1)}, f32[3,3,1,1032]{3,2,1,0:T(1,128)S(1)}, u32[]{:S(2)}, u32[]{:S(2)}) collective-permute-start(f32[3,3,1,1032]{3,2,1,0:T(1,128)S(1)} %get-tuple-element.5), channel_id=1, source_target_pairs={{0,4},{4,8},{8,12},{12,16},{16,20},{20,24},{24,28},{1,5},{5,9},{9,... | collective-permute-start | bytes 111464 | tf_op jit(solution)/shard_map/ppermute | solution.py:14
  230.7 5.9 %collective-permute-start.3 = (f32[3,3,1,1032]{3,2,1,0:T(1,128)S(1)}, f32[3,3,1,1032]{3,2,1,0:T(1,128)S(1)}, u32[]{:S(2)}, u32[]{:S(2)}) collective-permute-start(f32[3,3,1,1032]{3,2,1,0:T(1,128)S(1)} %get-tuple-element.6), channel_id=1, source_target_pairs={{4,0},{8,4},{12,8},{16,12},{20,16},{24,20},{28,24},{5,1},{9,5},{13... | collective-permute-start | bytes 111464 | tf_op jit(solution)/shard_map/ppermute | solution.py:17
  237.8 14.5 %collective-permute-start.4 = (f32[3,1,34,1032]{3,2,1,0:T(8,128)}, f32[3,1,34,1032]{3,2,1,0:T(8,128)}, u32[]{:S(2)}, u32[]{:S(2)}) collective-permute-start(f32[3,1,34,1032]{3,2,1,0:T(8,128)} %get-tuple-element.21), channel_id=1, source_target_pairs={{0,1},{2,3},{4,5},{6,7},{8,9},{10,11},{12,13},{14,15},{16,17},{18,... | collective-permute-start | bytes 1263176 | tf_op jit(solution)/shard_map/ppermute | solution.py:14
  241.9 15.2 %collective-permute-start.5 = (f32[3,1,34,1032]{3,2,1,0:T(8,128)}, f32[3,1,34,1032]{3,2,1,0:T(8,128)}, u32[]{:S(2)}, u32[]{:S(2)}) collective-permute-start(f32[3,1,34,1032]{3,2,1,0:T(8,128)} %get-tuple-element.22), channel_id=1, source_target_pairs={{1,0},{3,2},{5,4},{7,6},{9,8},{11,10},{13,12},{15,14},{17,16},{19,... | collective-permute-start | bytes 1263176 | tf_op jit(solution)/shard_map/ppermute | solution.py:17
  243.4 2.8 collective-permute-start
  244.7 3.4 collective-permute-start.1
  263.9 6.1 %collective-permute-start.6 = (f32[3,3,1,1032]{3,2,1,0:T(1,128)S(1)}, f32[3,3,1,1032]{3,2,1,0:T(1,128)S(1)}, u32[]{:S(2)}, u32[]{:S(2)}) collective-permute-start(f32[3,3,1,1032]{3,2,1,0:T(1,128)S(1)} %get-tuple-element.27), channel_id=1, source_target_pairs={{0,4},{4,8},{8,12},{12,16},{16,20},{20,24},{24,28},{1,5},{5,9},{9,... | collective-permute-start | bytes 111464 | tf_op jit(solution)/shard_map/ppermute | solution.py:14
  268.2 5.9 %collective-permute-start.7 = (f32[3,3,1,1032]{3,2,1,0:T(1,128)S(1)}, f32[3,3,1,1032]{3,2,1,0:T(1,128)S(1)}, u32[]{:S(2)}, u32[]{:S(2)}) collective-permute-start(f32[3,3,1,1032]{3,2,1,0:T(1,128)S(1)} %get-tuple-element.28), channel_id=1, source_target_pairs={{4,0},{8,4},{12,8},{16,12},{20,16},{24,20},{28,24},{5,1},{9,5},{13... | collective-permute-start | bytes 111464 | tf_op jit(solution)/shard_map/ppermute | solution.py:17
  274.3 11.3 %collective-permute-start.8 = (f32[3,1,34,1032]{3,2,1,0:T(8,128)S(1)}, f32[3,1,34,1032]{3,2,1,0:T(8,128)S(1)}, u32[]{:S(2)}, u32[]{:S(2)}) collective-permute-start(f32[3,1,34,1032]{3,2,1,0:T(8,128)S(1)} %get-tuple-element.19), channel_id=1, source_target_pairs={{0,1},{2,3},{4,5},{6,7},{8,9},{10,11},{12,13},{14,15},{16,17},{18,... | collective-permute-start | bytes 1263176 | tf_op jit(solution)/shard_map/ppermute | solution.py:14
  275.8 14.0 %collective-permute-start.9 = (f32[3,1,34,1032]{3,2,1,0:T(8,128)S(1)}, f32[3,1,34,1032]{3,2,1,0:T(8,128)S(1)}, u32[]{:S(2)}, u32[]{:S(2)}) collective-permute-start(f32[3,1,34,1032]{3,2,1,0:T(8,128)S(1)} %get-tuple-element.20), channel_id=1, source_target_pairs={{1,0},{3,2},{5,4},{7,6},{9,8},{11,10},{13,12},{15,14},{17,16},{19,... | collective-permute-start | bytes 1263176 | tf_op jit(solution)/shard_map/ppermute | solution.py:17
  294.0 5.2 %collective-permute-start.10 = (f32[3,3,1,1032]{3,2,1,0:T(1,128)S(1)}, f32[3,3,1,1032]{3,2,1,0:T(1,128)S(1)}, u32[]{:S(2)}, u32[]{:S(2)}) collective-permute-start(f32[3,3,1,1032]{3,2,1,0:T(1,128)S(1)} %get-tuple-element.25), channel_id=1, source_target_pairs={{0,4},{4,8},{8,12},{12,16},{16,20},{20,24},{24,28},{1,5},{5,9},{9,... | collective-permute-start | bytes 111464 | tf_op jit(solution)/shard_map/ppermute | solution.py:14
  297.4 5.9 %collective-permute-start.11 = (f32[3,3,1,1032]{3,2,1,0:T(1,128)S(1)}, f32[3,3,1,1032]{3,2,1,0:T(1,128)S(1)}, u32[]{:S(2)}, u32[]{:S(2)}) collective-permute-start(f32[3,3,1,1032]{3,2,1,0:T(1,128)S(1)} %get-tuple-element.26), channel_id=1, source_target_pairs={{4,0},{8,4},{12,8},{16,12},{20,16},{24,20},{28,24},{5,1},{9,5},{13... | collective-permute-start | bytes 111464 | tf_op jit(solution)/shard_map/ppermute | solution.py:17
  303.4 8.9 %collective-permute-start.12 = (f32[3,1,34,1032]{3,2,1,0:T(8,128)S(1)}, f32[3,1,34,1032]{3,2,1,0:T(8,128)S(1)}, u32[]{:S(2)}, u32[]{:S(2)}) collective-permute-start(f32[3,1,34,1032]{3,2,1,0:T(8,128)S(1)} %get-tuple-element.17), channel_id=1, source_target_pairs={{0,1},{2,3},{4,5},{6,7},{8,9},{10,11},{12,13},{14,15},{16,17},{18,... | collective-permute-start | bytes 1263176 | tf_op jit(solution)/shard_map/ppermute | solution.py:14
  304.9 11.5 %collective-permute-start.13 = (f32[3,1,34,1032]{3,2,1,0:T(8,128)S(1)}, f32[3,1,34,1032]{3,2,1,0:T(8,128)S(1)}, u32[]{:S(2)}, u32[]{:S(2)}) collective-permute-start(f32[3,1,34,1032]{3,2,1,0:T(8,128)S(1)} %get-tuple-element.18), channel_id=1, source_target_pairs={{1,0},{3,2},{5,4},{7,6},{9,8},{11,10},{13,12},{15,14},{17,16},{19,... | collective-permute-start | bytes 1263176 | tf_op jit(solution)/shard_map/ppermute | solution.py:17
  320.7 6.0 %collective-permute-start.14 = (f32[3,3,1,1032]{3,2,1,0:T(1,128)S(1)}, f32[3,3,1,1032]{3,2,1,0:T(1,128)S(1)}, u32[]{:S(2)}, u32[]{:S(2)}) collective-permute-start(f32[3,3,1,1032]{3,2,1,0:T(1,128)S(1)} %get-tuple-element.23), channel_id=1, source_target_pairs={{0,4},{4,8},{8,12},{12,16},{16,20},{20,24},{24,28},{1,5},{5,9},{9,... | collective-permute-start | bytes 111464 | tf_op jit(solution)/shard_map/ppermute | solution.py:14
  325.1 5.9 %collective-permute-start.15 = (f32[3,3,1,1032]{3,2,1,0:T(1,128)S(1)}, f32[3,3,1,1032]{3,2,1,0:T(1,128)S(1)}, u32[]{:S(2)}, u32[]{:S(2)}) collective-permute-start(f32[3,3,1,1032]{3,2,1,0:T(1,128)S(1)} %get-tuple-element.24), channel_id=1, source_target_pairs={{4,0},{8,4},{12,8},{16,12},{20,16},{24,20},{28,24},{5,1},{9,5},{13... | collective-permute-start | bytes 111464 | tf_op jit(solution)/shard_map/ppermute | solution.py:17
  331.1 8.4 %collective-permute-start.16 = (f32[3,1,34,1032]{3,2,1,0:T(8,128)S(1)}, f32[3,1,34,1032]{3,2,1,0:T(8,128)S(1)}, u32[]{:S(2)}, u32[]{:S(2)}) collective-permute-start(f32[3,1,34,1032]{3,2,1,0:T(8,128)S(1)} %get-tuple-element.15), channel_id=1, source_target_pairs={{0,1},{2,3},{4,5},{6,7},{8,9},{10,11},{12,13},{14,15},{16,17},{18,... | collective-permute-start | bytes 1263176 | tf_op jit(solution)/shard_map/ppermute | solution.py:14
  332.6 11.4 %collective-permute-start.17 = (f32[3,1,34,1032]{3,2,1,0:T(8,128)S(1)}, f32[3,1,34,1032]{3,2,1,0:T(8,128)S(1)}, u32[]{:S(2)}, u32[]{:S(2)}) collective-permute-start(f32[3,1,34,1032]{3,2,1,0:T(8,128)S(1)} %get-tuple-element.16), channel_id=1, source_target_pairs={{1,0},{3,2},{5,4},{7,6},{9,8},{11,10},{13,12},{15,14},{17,16},{19,... | collective-permute-start | bytes 1263176 | tf_op jit(solution)/shard_map/ppermute | solution.py:17
  (9 other events, 39.4 us)
Sparse Core Ops, SparseCore 0:
  9.5 75.4 all-gather.2
  86.5 18.3 all-gather.4
  204.4 21.1 all-reduce.7
where the time goes:
time: 357 us; the launch traced here: 356 us
  waiting for transfers between devices  174 us (49%)
  blocking collectives  64.2 us (18%)
  starting transfers between devices  43.5 us (12%)
  local copies, waits for them, and re-layouts  30.2 us (8%)
  other arithmetic  25.1 us (7%)
  between operations  13.6 us (4%)
  matrix products  5.59 us (2%)
    all_gather x1, waiting for transfers between devices, on_device(): column_block = lax.all_gather(own_block, 'row', axis=0, tiled=True)  76.3 us
    all_gather x1, blocking collectives, on_device(): row_whole = lax.all_gather(row_taper, 'row', axis=0, tiled=True)  41.8 us
    ppermute x9, waiting for transfers between devices, extended(): lax.ppermute(lax.slice_in_dim(block, 0, width, axis=dim), axis, backward)  36.1 us
    ppermute x9, starting transfers between devices, extended(): lax.ppermute(lax.slice_in_dim(block, block.shape[dim] - width, None, axis...  25.5 us
    all_to_all x1, blocking collectives, on_device(): lax.all_to_all(tapered.astype(jnp.bfloat16), 'row', split_axis=1, concat_...  22.4 us
    ppermute x9, waiting for transfers between devices, extended(): lax.ppermute(lax.slice_in_dim(block, block.shape[dim] - width, None, axis...  21.8 us
    all_gather x1, waiting for transfers between devices, on_device(): lax.all_gather(column_block, 'mem', axis=1, tiled=True)  19.9 us
    psum x1, waiting for transfers between devices, on_device(): summed = lax.psum(weighted, 'mem')  19.7 us
  transfers between devices with their start and end apart: 22, of which 19 were waited for; matrix products, arithmetic and copies ran while one was open for 2% of the time, Pallas kernels for 0%

commit v1 on v0

--- a/solution.py
+++ b/solution.py
@@ -4,6 +4,15 @@
 from jax.sharding import PartitionSpec as P
 
 STEPS = 4
+
+
+def stacks_all_make(in_array, dim_i):
+    in_array = jnp.moveaxis(in_array, 0, dim_i)
+    carry_in = in_array.shape
+    mid_arr = in_array.reshape(
+        *carry_in[:dim_i], carry_in[dim_i] * carry_in[dim_i + 1], *carry_in[dim_i + 2 :]
+    )
+    return mid_arr
 
 
 def extended(block, sides, width):
@@ -51,7 +60,23 @@
     own_block = lax.dynamic_slice_in_dim(
         column_taper, lax.axis_index("mem") * block_width, block_width, 1
     )
-    column_block = lax.all_gather(own_block, "row", axis=0, tiled=True)
+    q_n = jax.lax.axis_size("row")
+    trail = [(rr, (rr + 1) % q_n) for rr in range(q_n)]
+    all_rows = [(i0, q) for q, i0 in trail]
+    nth = 0
+    v_now, front = ([], [])
+    while nth < q_n - 1:
+        if nth % 2 == 0:
+            v_now.append(jax.lax.ppermute(v_now[-1] if v_now else own_block, "row", trail))
+        else:
+            front.append(jax.lax.ppermute(front[-1] if front else own_block, "row", all_rows))
+        nth += 1
+    r_now = jnp.stack([*v_now[::-1], own_block, *front], axis=0)
+    tile_out = len(v_now)
+    outcome_arr = jax.lax.axis_index("row")
+    vec_out = outcome_arr - tile_out
+    r_now = r_now[(jnp.arange(q_n) - vec_out) % q_n]
+    column_block = stacks_all_make(r_now, 0)
     first_pass = jnp.dot(
         flattened,
         lax.all_gather(column_block, "mem", axis=1, tiled=True),

time: 357 us -> 380 us (1.064)
  starting transfers between devices: 43.5 us -> 82.6 us
  waiting for transfers between devices: 174 us -> 145 us
  local copies, waits for them, and re-layouts: 30.2 us -> 42.9 us
    all_gather x1 -> x0, waiting for transfers between devices: 76.3 us -> none  [on_device(): column_block = lax.all_gather(own_block, 'row', axis=0, tiled=True)]
    ppermute x0 -> x7, waiting for transfers between devices: none -> 49.7 us  [the longest x4 49.7 us: on_device(): jax.lax.ppermute(v_now[-1] if v_now else own_block, 'row', trail)]
    ppermute x0 -> x7, starting transfers between devices: none -> 38.4 us  [the longest x3 30.4 us: on_device(): jax.lax.ppermute(front[-1] if front else own_block, 'row', all_rows)]
    unnamed x25 -> x32, local copies, waits for them, and re-layouts: 14 us -> 19.8 us
    gather x0 -> x1, local copies, waits for them, and re-layouts: none -> 5.05 us  [on_device(): r_now = r_now[(jnp.arange(q_n) - vec_out) % q_n]]
  transfers between devices with their start and end apart: 22 -> 28, of which waited for: 19 -> 22; matrix products, arithmetic and copies ran while one was open for 2% -> 4% of each run, Pallas kernels for 0% -> 0%
where the time goes in v1:
time: 380 us; the launch traced here: 379 us
  waiting for transfers between devices  145 us (38%)
  starting transfers between devices  82.6 us (22%)
  blocking collectives  64.2 us (17%)
  local copies, waits for them, and re-layouts  42.9 us (11%)
  other arithmetic  24.7 us (6%)
  between operations  13.9 us (4%)
  matrix products  5.59 us (1%)
    ppermute x4, waiting for transfers between devices, on_device(): jax.lax.ppermute(v_now[-1] if v_now else own_block, 'row', trail)  49.7 us
    all_gather x1, blocking collectives, on_device(): row_whole = lax.all_gather(row_taper, 'row', axis=0, tiled=True)  41.8 us
    ppermute x9, waiting for transfers between devices, extended(): lax.ppermute(lax.slice_in_dim(block, 0, width, axis=dim), axis, backward)  32.4 us
    ppermute x3, starting transfers between devices, on_device(): jax.lax.ppermute(front[-1] if front else own_block, 'row', all_rows)  30.4 us
    ppermute x9, starting transfers between devices, extended(): lax.ppermute(lax.slice_in_dim(block, block.shape[dim] - width, None, axis...  26.2 us
    ppermute x9, waiting for transfers between devices, extended(): lax.ppermute(lax.slice_in_dim(block, block.shape[dim] - width, None, axis...  24.7 us
    all_to_all x1, blocking collectives, on_device(): lax.all_to_all(tapered.astype(jnp.bfloat16), 'row', split_axis=1, concat_...  22.4 us
    unnamed x32, local copies, waits for them, and re-layouts  19.8 us
  transfers between devices with their start and end apart: 28, of which 22 were waited for; matrix products, arithmetic and copies ran while one was open for 4% of the time, Pallas kernels for 0%

profile of v1, /device:TPU:0, one launch (start us, length us, event | category | flops | bytes accessed | tf_op | source)
XLA Modules:
  0.0 378.9 jit_solution(13636920325170489562)
XLA Ops:
  10.7 15.0 %collective-permute-done = bf16[256,1024]{1,0:T(8,128)(2,1)S(1)} collective-permute-done((bf16[256,1024]{1,0:T(8,128)(2,1)S(1)}, bf16[256,1024]{1,0:T(8,128)(2,1)S(1)}, u32[]{:S(2)}, u32[]{:S(2)}) %collective-permute-start) | collective-permute-done | bytes 524320 | tf_op jit(solution)/shard_map/ppermute | solution.py:70
  25.7 4.7 %collective-permute-start.4 = (bf16[256,1024]{1,0:T(8,128)(2,1)S(1)}, bf16[256,1024]{1,0:T(8,128)(2,1)S(1)}, u32[]{:S(2)}, u32[]{:S(2)}) collective-permute-start(bf16[256,1024]{1,0:T(8,128)(2,1)S(1)} %constant_dynamic-slice_fusion), channel_id=1, source_target_pairs={{4,0},{8,4},{12,8},{16,12},{20,16},{24,20},{28,24},{0,28},{5,1},{9... | collective-permute-start | bytes 1572872 | tf_op jit(solution)/shard_map/ppermute | solution.py:72
  30.4 17.4 %collective-permute-done.1 = bf16[256,1024]{1,0:T(8,128)(2,1)S(1)} collective-permute-done((bf16[256,1024]{1,0:T(8,128)(2,1)S(1)}, bf16[256,1024]{1,0:T(8,128)(2,1)S(1)}, u32[]{:S(2)}, u32[]{:S(2)}) %collective-permute-start.1) | collective-permute-done | bytes 524320 | tf_op jit(solution)/shard_map/ppermute | solution.py:70
  50.3 12.3 %collective-permute-start.5 = (bf16[256,1024]{1,0:T(8,128)(2,1)S(1)}, bf16[256,1024]{1,0:T(8,128)(2,1)S(1)}, u32[]{:S(2)}, u32[]{:S(2)}) collective-permute-start(bf16[256,1024]{1,0:T(8,128)(2,1)S(1)} %collective-permute-done.4), channel_id=1, source_target_pairs={{4,0},{8,4},{12,8},{16,12},{20,16},{24,20},{28,24},{0,28},{5,1},{9... | collective-permute-start | bytes 1572872 | tf_op jit(solution)/shard_map/ppermute | solution.py:72
  62.5 9.1 %collective-permute-done.2 = bf16[256,1024]{1,0:T(8,128)(2,1)S(1)} collective-permute-done((bf16[256,1024]{1,0:T(8,128)(2,1)S(1)}, bf16[256,1024]{1,0:T(8,128)(2,1)S(1)}, u32[]{:S(2)}, u32[]{:S(2)}) %collective-permute-start.2) | collective-permute-done | bytes 524320 | tf_op jit(solution)/shard_map/ppermute | solution.py:70
  74.2 13.4 %collective-permute-start.6 = (bf16[256,1024]{1,0:T(8,128)(2,1)S(1)}, bf16[256,1024]{1,0:T(8,128)(2,1)S(1)}, u32[]{:S(2)}, u32[]{:S(2)}) collective-permute-start(bf16[256,1024]{1,0:T(8,128)(2,1)S(1)} %collective-permute-done.5), channel_id=1, source_target_pairs={{4,0},{8,4},{12,8},{16,12},{20,16},{24,20},{28,24},{0,28},{5,1},{9... | collective-permute-start | bytes 1572872 | tf_op jit(solution)/shard_map/ppermute | solution.py:72
  87.6 8.2 %collective-permute-done.3 = bf16[256,1024]{1,0:T(8,128)(2,1)} collective-permute-done((bf16[256,1024]{1,0:T(8,128)(2,1)S(1)}, bf16[256,1024]{1,0:T(8,128)(2,1)}, u32[]{:S(2)}, u32[]{:S(2)}) %collective-permute-start.3) | collective-permute-done | bytes 524320 | tf_op jit(solution)/shard_map/ppermute | solution.py:70
  103.6 5.1 %gather_fusion = bf16[8,256,1024]{2,1,0:T(8,128)(2,1)} fusion(bf16[8,256,1024]{2,1,0:T(8,128)(2,1)} %bitcast_dynamic-update-slice_fusion, s32[1024]{0:T(1024)S(1)} %pad_clamp_fusion), kind=kCustom, calls=%fused_computation | custom fusion | bytes 8388640 | tf_op jit(solution)/shard_map/gather | solution.py:78
  108.7 18.5 %all-gather.2.cloned.1.call-done = bf16[2048,2048]{1,0:T(8,128)(2,1)} async-done(((bf16[2048,1024]{1,0:T(8,128)(2,1)}), bf16[2048,2048]{1,0:T(8,128)(2,1)}) %all-gather.2.cloned.1.call-update) | async-done | bytes 8388624 | tf_op jit(solution)/shard_map/all_gather | solution.py:82
  127.3 5.2 %convolution_convert_fusion = bf16[2048,192]{0,1:T(8,128)(2,1)S(1)} fusion(bf16[192,2048]{1,0:T(8,128)(2,1)S(1)} %bitcast.60, bf16[2048,2048]{1,0:T(8,128)(2,1)} %all-gather.2.cloned.1.call-done), kind=kOutput, calls=%fused_computation.24 | convolution fusion | flops 1611005952 | bytes 9961472 | tf_op jit(solution)/shard_map/dot_general | solution.py:80
  136.6 5.7 %reshape.77 = bf16[8,2,24576]{2,1,0:T(2,128)(2,1)} reshape(bf16[2048,6,32]{2,1,0:T(8,128)(2,1)} %bitcast.61) | data formatting | bytes 1572864
  142.3 5.9 %all-to-all-start = ((bf16[8,2,24576]{2,1,0:T(2,128)(2,1)}), bf16[8,2,24576]{2,1,0:T(2,128)(2,1)S(1)}, u32[]{:S(2)}, u32[]{:S(2)}) async-start(bf16[8,2,24576]{2,1,0:T(2,128)(2,1)} %reshape.77), calls=%async_computation | async-start | bytes 1572864 | tf_op jit(solution)/shard_map/all_to_all | solution.py:90
  148.3 41.8 %all_gather.7 = bf16[256,256]{1,0:T(8,128)(2,1)S(1)} all-gather(bf16[32,256]{1,0:T(8,128)(2,1)S(1)} %copy-done.10), channel_id=1, replica_groups=mesh['row'=8,'mem'=2,'lev'=2] {'row'}, dimensions={0}, use_global_device_ids=true | all-gather | bytes 147456 | tf_op jit(solution)/shard_map/all_gather | solution.py:86
  199.7 22.4 %all_to_all.33 = bf16[6,256,256]{2,0,1:T(8,128)(2,1)S(1)} all-to-all(bf16[6,256,256]{2,0,1:T(8,128)(2,1)S(1)} %copy.19), channel_id=1, replica_groups=mesh['row'=8,'mem'=2,'lev'=2] {'row'}, dimensions={1} | all-to-all | bytes 1572864 | tf_op jit(solution)/shard_map/all_to_all | solution.py:93
  228.2 19.7 %all-reduce.8.cloned.1.call-done = f32[3,3,32,2048]{3,2,1,0:T(8,128)} async-done(((f32[3,3,32,2048]{3,2,1,0:T(8,128)}), f32[3,3,32,2048]{3,2,1,0:T(8,128)}) %all-reduce.8.cloned.1.call-update) | async-done | bytes 2359312 | tf_op jit(solution)/shard_map/psum | solution.py:100
  250.7 4.5 %collective-permute-start.9 = (f32[3,3,1,1032]{3,2,1,0:T(1,128)S(1)}, f32[3,3,1,1032]{3,2,1,0:T(1,128)S(1)}, u32[]{:S(2)}, u32[]{:S(2)}) collective-permute-start(f32[3,3,1,1032]{3,2,1,0:T(1,128)S(1)} %get-tuple-element.5), channel_id=1, source_target_pairs={{0,4},{4,8},{8,12},{12,16},{16,20},{20,24},{24,28},{1,5},{5,9},{9,... | collective-permute-start | bytes 111464 | tf_op jit(solution)/shard_map/ppermute | solution.py:23
  283.8 4.3 %collective-permute-start.13 = (f32[3,3,1,1032]{3,2,1,0:T(1,128)S(1)}, f32[3,3,1,1032]{3,2,1,0:T(1,128)S(1)}, u32[]{:S(2)}, u32[]{:S(2)}) collective-permute-start(f32[3,3,1,1032]{3,2,1,0:T(1,128)S(1)} %get-tuple-element.27), channel_id=1, source_target_pairs={{0,4},{4,8},{8,12},{12,16},{16,20},{20,24},{24,28},{1,5},{5,9},{9,... | collective-permute-start | bytes 111464 | tf_op jit(solution)/shard_map/ppermute | solution.py:23
  289.7 5.1 %collective-permute-done.14 = f32[3,3,1,1032]{3,2,1,0:T(1,128)S(1)} collective-permute-done((f32[3,3,1,1032]{3,2,1,0:T(1,128)S(1)}, f32[3,3,1,1032]{3,2,1,0:T(1,128)S(1)}, u32[]{:S(2)}, u32[]{:S(2)}) %collective-permute-start.14) | collective-permute-done | bytes 37184 | tf_op jit(solution)/shard_map/ppermute | solution.py:26
  297.7 9.5 %collective-permute-done.15 = f32[3,1,34,1032]{3,2,1,0:T(8,128)S(1)} collective-permute-done((f32[3,1,34,1032]{3,2,1,0:T(8,128)S(1)}, f32[3,1,34,1032]{3,2,1,0:T(8,128)S(1)}, u32[]{:S(2)}, u32[]{:S(2)}) %collective-permute-start.15) | collective-permute-done | bytes 421088 | tf_op jit(solution)/shard_map/ppermute | solution.py:23
  315.6 4.5 %collective-permute-start.17 = (f32[3,3,1,1032]{3,2,1,0:T(1,128)S(1)}, f32[3,3,1,1032]{3,2,1,0:T(1,128)S(1)}, u32[]{:S(2)}, u32[]{:S(2)}) collective-permute-start(f32[3,3,1,1032]{3,2,1,0:T(1,128)S(1)} %get-tuple-element.25), channel_id=1, source_target_pairs={{0,4},{4,8},{8,12},{12,16},{16,20},{20,24},{24,28},{1,5},{5,9},{9,... | collective-permute-start | bytes 111464 | tf_op jit(solution)/shard_map/ppermute | solution.py:23
  321.8 4.2 %collective-permute-done.18 = f32[3,3,1,1032]{3,2,1,0:T(1,128)S(1)} collective-permute-done((f32[3,3,1,1032]{3,2,1,0:T(1,128)S(1)}, f32[3,3,1,1032]{3,2,1,0:T(1,128)S(1)}, u32[]{:S(2)}, u32[]{:S(2)}) %collective-permute-start.18) | collective-permute-done | bytes 37184 | tf_op jit(solution)/shard_map/ppermute | solution.py:26
  329.0 6.7 %collective-permute-done.19 = f32[3,1,34,1032]{3,2,1,0:T(8,128)S(1)} collective-permute-done((f32[3,1,34,1032]{3,2,1,0:T(8,128)S(1)}, f32[3,1,34,1032]{3,2,1,0:T(8,128)S(1)}, u32[]{:S(2)}, u32[]{:S(2)}) %collective-permute-start.19) | collective-permute-done | bytes 421088 | tf_op jit(solution)/shard_map/ppermute | solution.py:23
  356.6 5.4 %collective-permute-done.23 = f32[3,1,34,1032]{3,2,1,0:T(8,128)S(1)} collective-permute-done((f32[3,1,34,1032]{3,2,1,0:T(8,128)S(1)}, f32[3,1,34,1032]{3,2,1,0:T(8,128)S(1)}, u32[]{:S(2)}, u32[]{:S(2)}) %collective-permute-start.23) | collective-permute-done | bytes 421088 | tf_op jit(solution)/shard_map/ppermute | solution.py:23
  362.1 4.4 %collective-permute-done.24 = f32[3,1,34,1032]{3,2,1,0:T(8,128)S(1)} collective-permute-done((f32[3,1,34,1032]{3,2,1,0:T(8,128)S(1)}, f32[3,1,34,1032]{3,2,1,0:T(8,128)S(1)}, u32[]{:S(2)}, u32[]{:S(2)}) %collective-permute-start.24) | collective-permute-done | bytes 421088 | tf_op jit(solution)/shard_map/ppermute | solution.py:26
  (112 shorter events, 111.9 us)
Async XLA Ops:
  6.5 120.7 %all-gather.2.cloned.1.call-start = ((), (), s32[]{:S(2)}) async-start(), calls=%async_computation.2 | async-start | bytes 12582912 | tf_op jit(solution)/shard_map/all_gather | solution.py:82
  7.7 18.0 %collective-permute-start = (bf16[256,1024]{1,0:T(8,128)(2,1)S(1)}, bf16[256,1024]{1,0:T(8,128)(2,1)S(1)}, u32[]{:S(2)}, u32[]{:S(2)}) collective-permute-start(bf16[256,1024]{1,0:T(8,128)(2,1)S(1)} %constant_dynamic-slice_fusion), channel_id=1, source_target_pairs={{0,4},{4,8},{8,12},{12,16},{16,20},{20,24},{24,28},{28,0},{1,5},{5... | collective-permute-start | bytes 1572872 | tf_op jit(solution)/shard_map/ppermute | solution.py:70
  25.7 22.1 %collective-permute-start.1 = (bf16[256,1024]{1,0:T(8,128)(2,1)S(1)}, bf16[256,1024]{1,0:T(8,128)(2,1)S(1)}, u32[]{:S(2)}, u32[]{:S(2)}) collective-permute-start(bf16[256,1024]{1,0:T(8,128)(2,1)S(1)} %collective-permute-done), channel_id=1, source_target_pairs={{0,4},{4,8},{8,12},{12,16},{16,20},{20,24},{24,28},{28,0},{1,5},{5... | collective-permute-start | bytes 1572872 | tf_op jit(solution)/shard_map/ppermute | solution.py:70
  25.7 24.6 %collective-permute-start.4 = (bf16[256,1024]{1,0:T(8,128)(2,1)S(1)}, bf16[256,1024]{1,0:T(8,128)(2,1)S(1)}, u32[]{:S(2)}, u32[]{:S(2)}) collective-permute-start(bf16[256,1024]{1,0:T(8,128)(2,1)S(1)} %constant_dynamic-slice_fusion), channel_id=1, source_target_pairs={{4,0},{8,4},{12,8},{16,12},{20,16},{24,20},{28,24},{0,28},{5,1},{9... | collective-permute-start | bytes 1572872 | tf_op jit(solution)/shard_map/ppermute | solution.py:72
  47.8 23.9 %collective-permute-start.2 = (bf16[256,1024]{1,0:T(8,128)(2,1)S(1)}, bf16[256,1024]{1,0:T(8,128)(2,1)S(1)}, u32[]{:S(2)}, u32[]{:S(2)}) collective-permute-start(bf16[256,1024]{1,0:T(8,128)(2,1)S(1)} %collective-permute-done.1), channel_id=1, source_target_pairs={{0,4},{4,8},{8,12},{12,16},{16,20},{20,24},{24,28},{28,0},{1,5},{5... | collective-permute-start | bytes 1572872 | tf_op jit(solution)/shard_map/ppermute | solution.py:70
  50.3 23.9 %collective-permute-start.5 = (bf16[256,1024]{1,0:T(8,128)(2,1)S(1)}, bf16[256,1024]{1,0:T(8,128)(2,1)S(1)}, u32[]{:S(2)}, u32[]{:S(2)}) collective-permute-start(bf16[256,1024]{1,0:T(8,128)(2,1)S(1)} %collective-permute-done.4), channel_id=1, source_target_pairs={{4,0},{8,4},{12,8},{16,12},{20,16},{24,20},{28,24},{0,28},{5,1},{9... | collective-permute-start | bytes 1572872 | tf_op jit(solution)/shard_map/ppermute | solution.py:72
  71.7 24.1 %collective-permute-start.3 = (bf16[256,1024]{1,0:T(8,128)(2,1)S(1)}, bf16[256,1024]{1,0:T(8,128)(2,1)}, u32[]{:S(2)}, u32[]{:S(2)}) collective-permute-start(bf16[256,1024]{1,0:T(8,128)(2,1)S(1)} %collective-permute-done.2), channel_id=1, source_target_pairs={{0,4},{4,8},{8,12},{12,16},{16,20},{20,24},{24,28},{28,0},{1,5},{5... | collective-permute-start | bytes 1572872 | tf_op jit(solution)/shard_map/ppermute | solution.py:70
  74.2 28.6 %collective-permute-start.6 = (bf16[256,1024]{1,0:T(8,128)(2,1)S(1)}, bf16[256,1024]{1,0:T(8,128)(2,1)S(1)}, u32[]{:S(2)}, u32[]{:S(2)}) collective-permute-start(bf16[256,1024]{1,0:T(8,128)(2,1)S(1)} %collective-permute-done.5), channel_id=1, source_target_pairs={{4,0},{8,4},{12,8},{16,12},{20,16},{24,20},{28,24},{0,28},{5,1},{9... | collective-permute-start | bytes 1572872 | tf_op jit(solution)/shard_map/ppermute | solution.py:72
  142.3 47.8 %all-to-all-start = ((bf16[8,2,24576]{2,1,0:T(2,128)(2,1)}), bf16[8,2,24576]{2,1,0:T(2,128)(2,1)S(1)}, u32[]{:S(2)}, u32[]{:S(2)}) async-start(bf16[8,2,24576]{2,1,0:T(2,128)(2,1)} %reshape.77), calls=%async_computation | async-start | bytes 1572864 | tf_op jit(solution)/shard_map/all_to_all | solution.py:90
  148.2 99.7 %all-reduce.8.cloned.1.call-start = ((), (), s32[]{:S(2)}) async-start(), calls=%async_computation.3 | async-start | bytes 4718592 | tf_op jit(solution)/shard_map/psum | solution.py:100
  249.4 6.3 %collective-permute-start.10 = (f32[3,3,1,1032]{3,2,1,0:T(1,128)S(1)}, f32[3,3,1,1032]{3,2,1,0:T(1,128)S(1)}, u32[]{:S(2)}, u32[]{:S(2)}) collective-permute-start(f32[3,3,1,1032]{3,2,1,0:T(1,128)S(1)} %get-tuple-element.6), channel_id=1, source_target_pairs={{4,0},{8,4},{12,8},{16,12},{20,16},{24,20},{28,24},{5,1},{9,5},{13... | collective-permute-start | bytes 111464 | tf_op jit(solution)/shard_map/ppermute | solution.py:26
  250.7 6.2 %collective-permute-start.9 = (f32[3,3,1,1032]{3,2,1,0:T(1,128)S(1)}, f32[3,3,1,1032]{3,2,1,0:T(1,128)S(1)}, u32[]{:S(2)}, u32[]{:S(2)}) collective-permute-start(f32[3,3,1,1032]{3,2,1,0:T(1,128)S(1)} %get-tuple-element.5), channel_id=1, source_target_pairs={{0,4},{4,8},{8,12},{12,16},{16,20},{20,24},{24,28},{1,5},{5,9},{9,... | collective-permute-start | bytes 111464 | tf_op jit(solution)/shard_map/ppermute | solution.py:23
  258.0 15.1 %collective-permute-start.11 = (f32[3,1,34,1032]{3,2,1,0:T(8,128)}, f32[3,1,34,1032]{3,2,1,0:T(8,128)S(1)}, u32[]{:S(2)}, u32[]{:S(2)}) collective-permute-start(f32[3,1,34,1032]{3,2,1,0:T(8,128)} %get-tuple-element.21), channel_id=1, source_target_pairs={{0,1},{2,3},{4,5},{6,7},{8,9},{10,11},{12,13},{14,15},{16,17},{18,... | collective-permute-start | bytes 1263176 | tf_op jit(solution)/shard_map/ppermute | solution.py:23
  261.7 15.6 %collective-permute-start.12 = (f32[3,1,34,1032]{3,2,1,0:T(8,128)}, f32[3,1,34,1032]{3,2,1,0:T(8,128)}, u32[]{:S(2)}, u32[]{:S(2)}) collective-permute-start(f32[3,1,34,1032]{3,2,1,0:T(8,128)} %get-tuple-element.22), channel_id=1, source_target_pairs={{1,0},{3,2},{5,4},{7,6},{9,8},{11,10},{13,12},{15,14},{17,16},{19,... | collective-permute-start | bytes 1263176 | tf_op jit(solution)/shard_map/ppermute | solution.py:26
  283.8 5.9 %collective-permute-start.13 = (f32[3,3,1,1032]{3,2,1,0:T(1,128)S(1)}, f32[3,3,1,1032]{3,2,1,0:T(1,128)S(1)}, u32[]{:S(2)}, u32[]{:S(2)}) collective-permute-start(f32[3,3,1,1032]{3,2,1,0:T(1,128)S(1)} %get-tuple-element.27), channel_id=1, source_target_pairs={{0,4},{4,8},{8,12},{12,16},{16,20},{20,24},{24,28},{1,5},{5,9},{9,... | collective-permute-start | bytes 111464 | tf_op jit(solution)/shard_map/ppermute | solution.py:23
  288.1 6.8 %collective-permute-start.14 = (f32[3,3,1,1032]{3,2,1,0:T(1,128)S(1)}, f32[3,3,1,1032]{3,2,1,0:T(1,128)S(1)}, u32[]{:S(2)}, u32[]{:S(2)}) collective-permute-start(f32[3,3,1,1032]{3,2,1,0:T(1,128)S(1)} %get-tuple-element.28), channel_id=1, source_target_pairs={{4,0},{8,4},{12,8},{16,12},{20,16},{24,20},{28,24},{5,1},{9,5},{13... | collective-permute-start | bytes 111464 | tf_op jit(solution)/shard_map/ppermute | solution.py:26
  295.0 12.3 %collective-permute-start.15 = (f32[3,1,34,1032]{3,2,1,0:T(8,128)S(1)}, f32[3,1,34,1032]{3,2,1,0:T(8,128)S(1)}, u32[]{:S(2)}, u32[]{:S(2)}) collective-permute-start(f32[3,1,34,1032]{3,2,1,0:T(8,128)S(1)} %get-tuple-element.19), channel_id=1, source_target_pairs={{0,1},{2,3},{4,5},{6,7},{8,9},{10,11},{12,13},{14,15},{16,17},{18,... | collective-permute-start | bytes 1263176 | tf_op jit(solution)/shard_map/ppermute | solution.py:23
  296.4 14.9 %collective-permute-start.16 = (f32[3,1,34,1032]{3,2,1,0:T(8,128)S(1)}, f32[3,1,34,1032]{3,2,1,0:T(8,128)S(1)}, u32[]{:S(2)}, u32[]{:S(2)}) collective-permute-start(f32[3,1,34,1032]{3,2,1,0:T(8,128)S(1)} %get-tuple-element.20), channel_id=1, source_target_pairs={{1,0},{3,2},{5,4},{7,6},{9,8},{11,10},{13,12},{15,14},{17,16},{19,... | collective-permute-start | bytes 1263176 | tf_op jit(solution)/shard_map/ppermute | solution.py:26
  315.6 6.2 %collective-permute-start.17 = (f32[3,3,1,1032]{3,2,1,0:T(1,128)S(1)}, f32[3,3,1,1032]{3,2,1,0:T(1,128)S(1)}, u32[]{:S(2)}, u32[]{:S(2)}) collective-permute-start(f32[3,3,1,1032]{3,2,1,0:T(1,128)S(1)} %get-tuple-element.25), channel_id=1, source_target_pairs={{0,4},{4,8},{8,12},{12,16},{16,20},{20,24},{24,28},{1,5},{5,9},{9,... | collective-permute-start | bytes 111464 | tf_op jit(solution)/shard_map/ppermute | solution.py:23
  320.2 5.9 %collective-permute-start.18 = (f32[3,3,1,1032]{3,2,1,0:T(1,128)S(1)}, f32[3,3,1,1032]{3,2,1,0:T(1,128)S(1)}, u32[]{:S(2)}, u32[]{:S(2)}) collective-permute-start(f32[3,3,1,1032]{3,2,1,0:T(1,128)S(1)} %get-tuple-element.26), channel_id=1, source_target_pairs={{4,0},{8,4},{12,8},{16,12},{20,16},{24,20},{28,24},{5,1},{9,5},{13... | collective-permute-start | bytes 111464 | tf_op jit(solution)/shard_map/ppermute | solution.py:26
  326.2 9.5 %collective-permute-start.19 = (f32[3,1,34,1032]{3,2,1,0:T(8,128)S(1)}, f32[3,1,34,1032]{3,2,1,0:T(8,128)S(1)}, u32[]{:S(2)}, u32[]{:S(2)}) collective-permute-start(f32[3,1,34,1032]{3,2,1,0:T(8,128)S(1)} %get-tuple-element.17), channel_id=1, source_target_pairs={{0,1},{2,3},{4,5},{6,7},{8,9},{10,11},{12,13},{14,15},{16,17},{18,... | collective-permute-start | bytes 1263176 | tf_op jit(solution)/shard_map/ppermute | solution.py:23
  327.7 12.2 %collective-permute-start.20 = (f32[3,1,34,1032]{3,2,1,0:T(8,128)S(1)}, f32[3,1,34,1032]{3,2,1,0:T(8,128)S(1)}, u32[]{:S(2)}, u32[]{:S(2)}) collective-permute-start(f32[3,1,34,1032]{3,2,1,0:T(8,128)S(1)} %get-tuple-element.18), channel_id=1, source_target_pairs={{1,0},{3,2},{5,4},{7,6},{9,8},{11,10},{13,12},{15,14},{17,16},{19,... | collective-permute-start | bytes 1263176 | tf_op jit(solution)/shard_map/ppermute | solution.py:26
  353.6 8.4 %collective-permute-start.23 = (f32[3,1,34,1032]{3,2,1,0:T(8,128)S(1)}, f32[3,1,34,1032]{3,2,1,0:T(8,128)S(1)}, u32[]{:S(2)}, u32[]{:S(2)}) collective-permute-start(f32[3,1,34,1032]{3,2,1,0:T(8,128)S(1)} %get-tuple-element.15), channel_id=1, source_target_pairs={{0,1},{2,3},{4,5},{6,7},{8,9},{10,11},{12,13},{14,15},{16,17},{18,... | collective-permute-start | bytes 1263176 | tf_op jit(solution)/shard_map/ppermute | solution.py:23
  355.1 11.4 %collective-permute-start.24 = (f32[3,1,34,1032]{3,2,1,0:T(8,128)S(1)}, f32[3,1,34,1032]{3,2,1,0:T(8,128)S(1)}, u32[]{:S(2)}, u32[]{:S(2)}) collective-permute-start(f32[3,1,34,1032]{3,2,1,0:T(8,128)S(1)} %get-tuple-element.16), channel_id=1, source_target_pairs={{1,0},{3,2},{5,4},{7,6},{9,8},{11,10},{13,12},{15,14},{17,16},{19,... | collective-permute-start | bytes 1263176 | tf_op jit(solution)/shard_map/ppermute | solution.py:26
  (15 other events, 211.2 us)
Sparse Core Ops, SparseCore 0:
  108.8 18.3 all-gather.1
  226.7 21.1 all-reduce.7
